TPU v7x, 32 devices: a whole 2x2x4 slice. The times are simulated.
32 devices in a mesh: grp: 4 (over y, x), dev: 8 (over z, core).
Axes of the slice: x: 2, y: 2, z: 4, core: 2. Of those that a mesh axis runs over, the one named last changes fastest.
Arguments:
- examples: float32 [2048, 32768], P(('grp', 'dev'))
- labels: int32 [2048], P(('grp', 'dev')), may hold values from 0 to 1, as said below
Outputs:
- consensus: float32 [32768], replicated
- local_weights: float32 [32, 32768], P(('grp', 'dev'))
- dual_vars: float32 [32, 32768], P(('grp', 'dev'))
Inputs may be any that keep to these rules, and one draw needn't show every extreme that they name: `labels`: each example's class, 0 or 1.
All inputs are finite; a program needn't handle non-finite values.
Results may differ from a plain program's by a relative error of at most 0.00012.
Values sent between devices are 32-bit elements; how exact they have to be, the bound alone decides.
A program may use at most 64 MiB of HBM per device.

v0:
```python
import jax
import jax.numpy as jnp
from jax import lax
from jax.sharding import PartitionSpec as P

PROX = 3
ROUNDS = 4
step_size = 200.0
penalty = 0.005
thresh = 0.04


def shrink(values):
    return values - jnp.clip(values, -thresh, thresh)


def local_steps(examples, targets, weight_vector, consensus_point):
    for prox_index in range(PROX):
        label_margins = jnp.dot(examples, weight_vector, precision=lax.Precision.HIGHEST)
        primal_residual = jax.nn.sigmoid(label_margins) - targets
        loss_gradient = jnp.dot(primal_residual, examples, precision=lax.Precision.HIGHEST)
        weight_vector = (
            weight_vector - step_size * loss_gradient + step_size * penalty * consensus_point
        ) / (1.0 + step_size * penalty)
    return weight_vector


def per_device(examples, labels):
    members = lax.axis_size("grp") * lax.axis_size("dev")
    targets = labels.astype(jnp.float32)
    width = examples.shape[1]

    def one_round(round_index, carried):
        consensus, weight_vector, dual_vars = carried
        consensus_point = consensus - dual_vars
        weight_vector = local_steps(examples, targets, weight_vector, consensus_point)
        combined = weight_vector + dual_vars
        summed = lax.psum(combined, ("grp", "dev"))
        consensus = shrink(summed / members)
        dual_vars = dual_vars + weight_vector - consensus
        return (consensus, weight_vector, dual_vars)

    start = (
        jnp.zeros((width,), jnp.float32),
        jnp.zeros((width,), jnp.float32),
        jnp.zeros((width,), jnp.float32),
    )
    consensus, weight_vector, dual_vars = lax.fori_loop(0, ROUNDS, one_round, start)
    return (consensus, weight_vector[None, :], dual_vars[None, :])


def solution(mesh):
    placed = (P(("grp", "dev"), None), P(("grp", "dev")))
    return jax.shard_map(
        per_device,
        mesh=mesh,
        in_specs=placed,
        out_specs=(P(), P(("grp", "dev"), None), P(("grp", "dev"), None)),
        check_vma=False,
    )
```

profile of v0, /device:TPU:0, one launch (start us, length us, event | category | flops | bytes accessed | tf_op | source)
XLA Modules:
  0.0 658.6 jit_solution(14624794344501646285)
XLA Ops:
  7.2 0.7 convert_element_type.3
  7.8 643.4 %while.15 = (s32[]{:T(128)}, f32[32768]{0:T(1024)S(1)}, f32[32768]{0:T(1024)S(1)}, f32[32768]{0:T(1024)S(1)}, f32[64,32768]{1,0:T(8,128)}, /*index=5*/f32[64]{0:T(128)S(1)}, s32[]{:T(128)}, s32[]{:T(128)}) while((s32[]{:T(128)}, f32[32768]{0:T(1024)S(1)}, f32[32768]{0:T(1024)S(1)}, f32[32768]{0:T(1024)S(1)}, ...), condition=%wide.region_2.3_spmd.clone, body=%wide.region_0.2_spmd.clone.sunk | while | flops 151782144 | bytes 88344992 | solution.py:48
  7.9 9.1 %fusion.65 = f32[64,1]{0,1:T(1,128)S(1)} fusion(f32[64]{0:T(128)S(1)} %get-tuple-element.149, f32[64,32768]{1,0:T(8,128)} %get-tuple-element.148, f32[32768,1]{0,1:T(1,128)S(1)} %bitcast.118), kind=kOutput, calls=%fused_computation.20.clone.1 | convolution fusion | flops 25166080 | bytes 8520192 | tf_op jit(solution)/shard_map/while/body/eval_jaxpr/dot_general | solution.py:19
  16.9 4.0 fusion.66
  21.0 6.6 fusion.67
  27.6 4.1 fusion.68
  31.7 6.6 fusion.69
  38.3 4.1 fusion.70
  42.3 0.7 select_add_fusion.2
  43.0 0.0 all-reduce.2.cloned.1.call-update
  43.0 127.3 %all-reduce.2.cloned.1.call-done = f32[32768]{0:T(1024)} async-done(((f32[32768]{0:T(1024)}), f32[32768]{0:T(1024)}) %all-reduce.2.cloned.1.call-update) | async-done | bytes 131088 | tf_op jit(solution)/shard_map/while/body/eval_jaxpr/psum | solution.py:38
  170.4 1.0 fusion.71
  171.4 0.0 all-reduce.2.cloned.1.call-start
  171.5 9.1 %fusion.65 = f32[64,1]{0,1:T(1,128)S(1)} fusion(f32[64]{0:T(128)S(1)} %get-tuple-element.149, f32[64,32768]{1,0:T(8,128)} %get-tuple-element.148, f32[32768,1]{0,1:T(1,128)S(1)} %bitcast.118), kind=kOutput, calls=%fused_computation.20.clone.1 | convolution fusion | flops 25166080 | bytes 8520192 | tf_op jit(solution)/shard_map/while/body/eval_jaxpr/dot_general | solution.py:19
  180.5 4.0 fusion.66
  184.6 6.6 fusion.67
  191.2 4.1 fusion.68
  195.3 6.6 fusion.69
  201.9 4.1 fusion.70
  205.9 0.7 select_add_fusion.2
  206.6 0.0 all-reduce.2.cloned.1.call-update
  206.6 123.7 %all-reduce.2.cloned.1.call-done = f32[32768]{0:T(1024)} async-done(((f32[32768]{0:T(1024)}), f32[32768]{0:T(1024)}) %all-reduce.2.cloned.1.call-update) | async-done | bytes 131088 | tf_op jit(solution)/shard_map/while/body/eval_jaxpr/psum | solution.py:38
  330.3 1.0 fusion.71
  331.3 0.0 all-reduce.2.cloned.1.call-start
  331.4 9.1 %fusion.65 = f32[64,1]{0,1:T(1,128)S(1)} fusion(f32[64]{0:T(128)S(1)} %get-tuple-element.149, f32[64,32768]{1,0:T(8,128)} %get-tuple-element.148, f32[32768,1]{0,1:T(1,128)S(1)} %bitcast.118), kind=kOutput, calls=%fused_computation.20.clone.1 | convolution fusion | flops 25166080 | bytes 8520192 | tf_op jit(solution)/shard_map/while/body/eval_jaxpr/dot_general | solution.py:19
  340.5 4.0 fusion.66
  344.6 6.6 fusion.67
  351.2 4.1 fusion.68
  355.3 6.6 fusion.69
  361.8 4.1 fusion.70
  365.9 0.7 select_add_fusion.2
  366.6 0.0 all-reduce.2.cloned.1.call-update
  366.6 123.7 %all-reduce.2.cloned.1.call-done = f32[32768]{0:T(1024)} async-done(((f32[32768]{0:T(1024)}), f32[32768]{0:T(1024)}) %all-reduce.2.cloned.1.call-update) | async-done | bytes 131088 | tf_op jit(solution)/shard_map/while/body/eval_jaxpr/psum | solution.py:38
  490.3 1.0 fusion.71
  491.3 0.0 all-reduce.2.cloned.1.call-start
  491.4 9.1 %fusion.65 = f32[64,1]{0,1:T(1,128)S(1)} fusion(f32[64]{0:T(128)S(1)} %get-tuple-element.149, f32[64,32768]{1,0:T(8,128)} %get-tuple-element.148, f32[32768,1]{0,1:T(1,128)S(1)} %bitcast.118), kind=kOutput, calls=%fused_computation.20.clone.1 | convolution fusion | flops 25166080 | bytes 8520192 | tf_op jit(solution)/shard_map/while/body/eval_jaxpr/dot_general | solution.py:19
  500.5 4.0 fusion.66
  504.6 6.6 fusion.67
  511.1 4.1 fusion.68
  515.2 6.6 fusion.69
  521.8 4.1 fusion.70
  525.9 0.7 select_add_fusion.2
  526.6 0.0 all-reduce.2.cloned.1.call-update
  526.6 123.7 %all-reduce.2.cloned.1.call-done = f32[32768]{0:T(1024)} async-done(((f32[32768]{0:T(1024)}), f32[32768]{0:T(1024)}) %all-reduce.2.cloned.1.call-update) | async-done | bytes 131088 | tf_op jit(solution)/shard_map/while/body/eval_jaxpr/psum | solution.py:38
  650.3 1.0 fusion.71
  651.3 0.6 copy-done.1
  651.9 0.0 copy-done.2
  652.0 0.0 copy-done.3
  (27 shorter events, 0.4 us)
Async XLA Ops:
  7.8 162.5 %all-reduce.2.cloned.1.call-start = ((), (), s32[]{:S(2)}) async-start(), calls=%async_computation | async-start | bytes 262144 | tf_op jit(solution)/shard_map/while/body/eval_jaxpr/psum | solution.py:38
  7.8 9.1 %copy-start = (f32[64,32768]{1,0:T(8,128)S(1)}, f32[64,32768]{1,0:T(8,128)}, u32[]{:S(2)}) copy-start(f32[64,32768]{1,0:T(8,128)} %get-tuple-element.148) | copy-start | bytes 25165828 | tf_op jit(solution)/shard_map/while
  171.4 159.0 %all-reduce.2.cloned.1.call-start = ((), (), s32[]{:S(2)}) async-start(), calls=%async_computation | async-start | bytes 262144 | tf_op jit(solution)/shard_map/while/body/eval_jaxpr/psum | solution.py:38
  171.4 9.1 %copy-start = (f32[64,32768]{1,0:T(8,128)S(1)}, f32[64,32768]{1,0:T(8,128)}, u32[]{:S(2)}) copy-start(f32[64,32768]{1,0:T(8,128)} %get-tuple-element.148) | copy-start | bytes 25165828 | tf_op jit(solution)/shard_map/while
  331.3 159.0 %all-reduce.2.cloned.1.call-start = ((), (), s32[]{:S(2)}) async-start(), calls=%async_computation | async-start | bytes 262144 | tf_op jit(solution)/shard_map/while/body/eval_jaxpr/psum | solution.py:38
  331.4 9.1 %copy-start = (f32[64,32768]{1,0:T(8,128)S(1)}, f32[64,32768]{1,0:T(8,128)}, u32[]{:S(2)}) copy-start(f32[64,32768]{1,0:T(8,128)} %get-tuple-element.148) | copy-start | bytes 25165828 | tf_op jit(solution)/shard_map/while
  491.3 159.0 %all-reduce.2.cloned.1.call-start = ((), (), s32[]{:S(2)}) async-start(), calls=%async_computation | async-start | bytes 262144 | tf_op jit(solution)/shard_map/while/body/eval_jaxpr/psum | solution.py:38
  491.4 9.1 %copy-start = (f32[64,32768]{1,0:T(8,128)S(1)}, f32[64,32768]{1,0:T(8,128)}, u32[]{:S(2)}) copy-start(f32[64,32768]{1,0:T(8,128)} %get-tuple-element.148) | copy-start | bytes 25165828 | tf_op jit(solution)/shard_map/while
  651.3 0.7 copy-start.1
  651.3 0.7 copy-start.2
  651.3 0.7 copy-start.3
Sparse Core Ops, SparseCore 0:
  43.2 127.1 all-reduce.1
  206.8 123.5 all-reduce.1
  366.7 123.5 all-reduce.1
  526.7 123.5 all-reduce.1
where the time goes:
time: 659 us
  waiting for transfers between devices  498 us (76%)
  matrix products  137 us (21%)
  between operations  13.7 us (2%)
  other arithmetic  7.74 us (1%)
    psum x4, waiting for transfers between devices, one_round(): summed = lax.psum(combined, ('grp', 'dev'))  498 us
    dot_general x12, matrix products, local_steps(): jnp.dot(examples, weight_vector, precision=lax.Precision.HIGHEST)  88.9 us
    dot_general x12, matrix products, local_steps(): jnp.dot(primal_residual, examples, precision=lax.Precision.HIGHEST)  48.6 us
  transfers between devices with their start and end apart: 4, of which 4 were waited for; matrix products, arithmetic and copies ran while one was open for 0% of the time, Pallas kernels for 0%

commit v1 on v0

--- a/solution.py
+++ b/solution.py
@@ -35,7 +35,7 @@
         consensus_point = consensus - dual_vars
         weight_vector = local_steps(examples, targets, weight_vector, consensus_point)
         combined = weight_vector + dual_vars
-        summed = lax.psum(combined, ("grp", "dev"))
+        summed = lax.psum(lax.psum(combined, "dev"), "grp")
         consensus = shrink(summed / members)
         dual_vars = dual_vars + weight_vector - consensus
         return (consensus, weight_vector, dual_vars)

time: 659 us -> 560 us (0.85)
  waiting for transfers between devices: 498 us -> 399 us
    psum x4 -> x8, waiting for transfers between devices: 498 us -> 399 us  [one_round(): summed = lax.psum(lax.psum(combined, 'dev'), 'grp')]
  transfers between devices with their start and end apart: 4 -> 8, of which waited for: 4 -> 8; matrix products, arithmetic and copies ran while one was open for 0% -> 0% of each run, Pallas kernels for 0% -> 0%
where the time goes in v1:
time: 560 us
  waiting for transfers between devices  399 us (71%)
  matrix products  137 us (24%)
  between operations  14 us (2%)
  other arithmetic  7.75 us (1%)
    psum x8, waiting for transfers between devices, one_round(): summed = lax.psum(lax.psum(combined, 'dev'), 'grp')  399 us
    dot_general x12, matrix products, local_steps(): jnp.dot(examples, weight_vector, precision=lax.Precision.HIGHEST)  88.9 us
    dot_general x12, matrix products, local_steps(): jnp.dot(primal_residual, examples, precision=lax.Precision.HIGHEST)  48.6 us
  transfers between devices with their start and end apart: 8, of which 8 were waited for; matrix products, arithmetic and copies ran while one was open for 0% of the time, Pallas kernels for 0%

profile of v1, /device:TPU:0, one launch (start us, length us, event | category | flops | bytes accessed | tf_op | source)
XLA Modules:
  0.0 559.9 jit_solution(9906690326476025602)
XLA Ops:
  7.2 0.7 convert_element_type.3
  7.8 544.5 %while.15 = (s32[]{:T(128)}, f32[32768]{0:T(1024)S(1)}, f32[32768]{0:T(1024)S(1)}, f32[32768]{0:T(1024)S(1)}, f32[64,32768]{1,0:T(8,128)}, /*index=5*/f32[64]{0:T(128)S(1)}, s32[]{:T(128)}, s32[]{:T(128)}) while((s32[]{:T(128)}, f32[32768]{0:T(1024)S(1)}, f32[32768]{0:T(1024)S(1)}, f32[32768]{0:T(1024)S(1)}, ...), condition=%wide.region_3.4_spmd.clone, body=%wide.region_0.3_spmd.clone.sunk | while | flops 151814912 | bytes 89131464 | solution.py:48
  7.9 9.1 %fusion.65 = f32[64,1]{0,1:T(1,128)S(1)} fusion(f32[64]{0:T(128)S(1)} %get-tuple-element.149, f32[64,32768]{1,0:T(8,128)} %get-tuple-element.148, f32[32768,1]{0,1:T(1,128)S(1)} %bitcast.118), kind=kOutput, calls=%fused_computation.20.clone.1 | convolution fusion | flops 25166080 | bytes 8520192 | tf_op jit(solution)/shard_map/while/body/eval_jaxpr/dot_general | solution.py:19
  16.9 4.0 fusion.66
  21.0 6.6 %fusion.67 = f32[64,1]{0,1:T(1,128)S(1)} fusion(f32[64]{0:T(128)S(1)} %get-tuple-element.149, f32[32768,1]{0,1:T(1,128)S(1)} %bitcast.117, f32[64,32768]{1,0:T(8,128)S(1)} %copy-done), kind=kOutput, calls=%fused_computation.13.clone.1 | convolution fusion | flops 25166080 | bytes 8520192 | tf_op jit(solution)/shard_map/while/body/eval_jaxpr/dot_general | solution.py:19
  27.6 4.1 fusion.68
  31.7 6.6 %fusion.69 = f32[64,1]{0,1:T(1,128)S(1)} fusion(f32[64]{0:T(128)S(1)} %get-tuple-element.149, f32[32768,1]{0,1:T(1,128)S(1)} %bitcast.116, f32[64,32768]{1,0:T(8,128)S(1)} %copy-done), kind=kOutput, calls=%fused_computation.6.clone.1 | convolution fusion | flops 25166080 | bytes 8520192 | tf_op jit(solution)/shard_map/while/body/eval_jaxpr/dot_general | solution.py:19
  38.3 4.1 fusion.70
  42.3 0.7 select_add_fusion.2
  43.1 57.8 %all-reduce.3.cloned.1.call-done = f32[32768]{0:T(1024)} async-done(((f32[32768]{0:T(1024)}), f32[32768]{0:T(1024)}) %all-reduce.3.cloned.1.call-update) | async-done | bytes 131088 | tf_op jit(solution)/shard_map/while/body/eval_jaxpr/psum | solution.py:38
  100.9 44.2 %all-reduce.5.cloned.1.call-done = f32[32768]{0:T(1024)} async-done(((f32[32768]{0:T(1024)}), f32[32768]{0:T(1024)}) %all-reduce.5.cloned.1.call-update) | async-done | bytes 131088 | tf_op jit(solution)/shard_map/while/body/eval_jaxpr/psum | solution.py:38
  145.0 1.0 fusion.71
  146.0 0.0 all-reduce.3.cloned.1.call-start
  146.1 9.1 %fusion.65 = f32[64,1]{0,1:T(1,128)S(1)} fusion(f32[64]{0:T(128)S(1)} %get-tuple-element.149, f32[64,32768]{1,0:T(8,128)} %get-tuple-element.148, f32[32768,1]{0,1:T(1,128)S(1)} %bitcast.118), kind=kOutput, calls=%fused_computation.20.clone.1 | convolution fusion | flops 25166080 | bytes 8520192 | tf_op jit(solution)/shard_map/while/body/eval_jaxpr/dot_general | solution.py:19
  155.2 4.0 fusion.66
  159.3 6.6 %fusion.67 = f32[64,1]{0,1:T(1,128)S(1)} fusion(f32[64]{0:T(128)S(1)} %get-tuple-element.149, f32[32768,1]{0,1:T(1,128)S(1)} %bitcast.117, f32[64,32768]{1,0:T(8,128)S(1)} %copy-done), kind=kOutput, calls=%fused_computation.13.clone.1 | convolution fusion | flops 25166080 | bytes 8520192 | tf_op jit(solution)/shard_map/while/body/eval_jaxpr/dot_general | solution.py:19
  165.9 4.1 fusion.68
  170.0 6.6 %fusion.69 = f32[64,1]{0,1:T(1,128)S(1)} fusion(f32[64]{0:T(128)S(1)} %get-tuple-element.149, f32[32768,1]{0,1:T(1,128)S(1)} %bitcast.116, f32[64,32768]{1,0:T(8,128)S(1)} %copy-done), kind=kOutput, calls=%fused_computation.6.clone.1 | convolution fusion | flops 25166080 | bytes 8520192 | tf_op jit(solution)/shard_map/while/body/eval_jaxpr/dot_general | solution.py:19
  176.6 4.1 fusion.70
  180.6 0.7 select_add_fusion.2
  181.4 55.0 %all-reduce.3.cloned.1.call-done = f32[32768]{0:T(1024)} async-done(((f32[32768]{0:T(1024)}), f32[32768]{0:T(1024)}) %all-reduce.3.cloned.1.call-update) | async-done | bytes 131088 | tf_op jit(solution)/shard_map/while/body/eval_jaxpr/psum | solution.py:38
  236.4 44.0 %all-reduce.5.cloned.1.call-done = f32[32768]{0:T(1024)} async-done(((f32[32768]{0:T(1024)}), f32[32768]{0:T(1024)}) %all-reduce.5.cloned.1.call-update) | async-done | bytes 131088 | tf_op jit(solution)/shard_map/while/body/eval_jaxpr/psum | solution.py:38
  280.4 1.0 fusion.71
  281.4 0.0 all-reduce.3.cloned.1.call-start
  281.5 9.1 %fusion.65 = f32[64,1]{0,1:T(1,128)S(1)} fusion(f32[64]{0:T(128)S(1)} %get-tuple-element.149, f32[64,32768]{1,0:T(8,128)} %get-tuple-element.148, f32[32768,1]{0,1:T(1,128)S(1)} %bitcast.118), kind=kOutput, calls=%fused_computation.20.clone.1 | convolution fusion | flops 25166080 | bytes 8520192 | tf_op jit(solution)/shard_map/while/body/eval_jaxpr/dot_general | solution.py:19
  290.6 4.0 fusion.66
  294.7 6.6 %fusion.67 = f32[64,1]{0,1:T(1,128)S(1)} fusion(f32[64]{0:T(128)S(1)} %get-tuple-element.149, f32[32768,1]{0,1:T(1,128)S(1)} %bitcast.117, f32[64,32768]{1,0:T(8,128)S(1)} %copy-done), kind=kOutput, calls=%fused_computation.13.clone.1 | convolution fusion | flops 25166080 | bytes 8520192 | tf_op jit(solution)/shard_map/while/body/eval_jaxpr/dot_general | solution.py:19
  301.3 4.1 fusion.68
  305.3 6.6 %fusion.69 = f32[64,1]{0,1:T(1,128)S(1)} fusion(f32[64]{0:T(128)S(1)} %get-tuple-element.149, f32[32768,1]{0,1:T(1,128)S(1)} %bitcast.116, f32[64,32768]{1,0:T(8,128)S(1)} %copy-done), kind=kOutput, calls=%fused_computation.6.clone.1 | convolution fusion | flops 25166080 | bytes 8520192 | tf_op jit(solution)/shard_map/while/body/eval_jaxpr/dot_general | solution.py:19
  311.9 4.1 fusion.70
  316.0 0.7 select_add_fusion.2
  316.7 55.0 %all-reduce.3.cloned.1.call-done = f32[32768]{0:T(1024)} async-done(((f32[32768]{0:T(1024)}), f32[32768]{0:T(1024)}) %all-reduce.3.cloned.1.call-update) | async-done | bytes 131088 | tf_op jit(solution)/shard_map/while/body/eval_jaxpr/psum | solution.py:38
  371.8 44.0 %all-reduce.5.cloned.1.call-done = f32[32768]{0:T(1024)} async-done(((f32[32768]{0:T(1024)}), f32[32768]{0:T(1024)}) %all-reduce.5.cloned.1.call-update) | async-done | bytes 131088 | tf_op jit(solution)/shard_map/while/body/eval_jaxpr/psum | solution.py:38
  415.8 1.0 fusion.71
  416.8 0.0 all-reduce.3.cloned.1.call-start
  416.9 9.1 %fusion.65 = f32[64,1]{0,1:T(1,128)S(1)} fusion(f32[64]{0:T(128)S(1)} %get-tuple-element.149, f32[64,32768]{1,0:T(8,128)} %get-tuple-element.148, f32[32768,1]{0,1:T(1,128)S(1)} %bitcast.118), kind=kOutput, calls=%fused_computation.20.clone.1 | convolution fusion | flops 25166080 | bytes 8520192 | tf_op jit(solution)/shard_map/while/body/eval_jaxpr/dot_general | solution.py:19
  426.0 4.0 fusion.66
  430.0 6.6 %fusion.67 = f32[64,1]{0,1:T(1,128)S(1)} fusion(f32[64]{0:T(128)S(1)} %get-tuple-element.149, f32[32768,1]{0,1:T(1,128)S(1)} %bitcast.117, f32[64,32768]{1,0:T(8,128)S(1)} %copy-done), kind=kOutput, calls=%fused_computation.13.clone.1 | convolution fusion | flops 25166080 | bytes 8520192 | tf_op jit(solution)/shard_map/while/body/eval_jaxpr/dot_general | solution.py:19
  436.6 4.1 fusion.68
  440.7 6.6 %fusion.69 = f32[64,1]{0,1:T(1,128)S(1)} fusion(f32[64]{0:T(128)S(1)} %get-tuple-element.149, f32[32768,1]{0,1:T(1,128)S(1)} %bitcast.116, f32[64,32768]{1,0:T(8,128)S(1)} %copy-done), kind=kOutput, calls=%fused_computation.6.clone.1 | convolution fusion | flops 25166080 | bytes 8520192 | tf_op jit(solution)/shard_map/while/body/eval_jaxpr/dot_general | solution.py:19
  447.3 4.1 fusion.70
  451.3 0.7 select_add_fusion.2
  452.1 55.0 %all-reduce.3.cloned.1.call-done = f32[32768]{0:T(1024)} async-done(((f32[32768]{0:T(1024)}), f32[32768]{0:T(1024)}) %all-reduce.3.cloned.1.call-update) | async-done | bytes 131088 | tf_op jit(solution)/shard_map/while/body/eval_jaxpr/psum | solution.py:38
  507.1 44.2 %all-reduce.5.cloned.1.call-done = f32[32768]{0:T(1024)} async-done(((f32[32768]{0:T(1024)}), f32[32768]{0:T(1024)}) %all-reduce.5.cloned.1.call-update) | async-done | bytes 131088 | tf_op jit(solution)/shard_map/while/body/eval_jaxpr/psum | solution.py:38
  551.3 1.0 fusion.71
  552.3 0.6 copy-done.1
  553.0 0.0 copy-done.2
  553.0 0.0 copy-done.3
  (39 shorter events, 0.7 us)
Async XLA Ops:
  7.8 93.0 %all-reduce.3.cloned.1.call-start = ((), (), s32[]{:S(2)}) async-start(), calls=%async_computation | async-start | bytes 262144 | tf_op jit(solution)/shard_map/while/body/eval_jaxpr/psum | solution.py:38
  7.8 9.1 %copy-start = (f32[64,32768]{1,0:T(8,128)S(1)}, f32[64,32768]{1,0:T(8,128)}, u32[]{:S(2)}) copy-start(f32[64,32768]{1,0:T(8,128)} %get-tuple-element.148) | copy-start | bytes 25165828 | tf_op jit(solution)/shard_map/while
  43.0 102.0 %all-reduce.5.cloned.1.call-start = ((), (), s32[]{:S(2)}) async-start(), calls=%async_computation.1 | async-start | bytes 262144 | tf_op jit(solution)/shard_map/while/body/eval_jaxpr/psum | solution.py:38
  146.0 90.3 %all-reduce.3.cloned.1.call-start = ((), (), s32[]{:S(2)}) async-start(), calls=%async_computation | async-start | bytes 262144 | tf_op jit(solution)/shard_map/while/body/eval_jaxpr/psum | solution.py:38
  146.1 9.1 %copy-start = (f32[64,32768]{1,0:T(8,128)S(1)}, f32[64,32768]{1,0:T(8,128)}, u32[]{:S(2)}) copy-start(f32[64,32768]{1,0:T(8,128)} %get-tuple-element.148) | copy-start | bytes 25165828 | tf_op jit(solution)/shard_map/while
  181.3 99.1 %all-reduce.5.cloned.1.call-start = ((), (), s32[]{:S(2)}) async-start(), calls=%async_computation.1 | async-start | bytes 262144 | tf_op jit(solution)/shard_map/while/body/eval_jaxpr/psum | solution.py:38
  281.4 90.3 %all-reduce.3.cloned.1.call-start = ((), (), s32[]{:S(2)}) async-start(), calls=%async_computation | async-start | bytes 262144 | tf_op jit(solution)/shard_map/while/body/eval_jaxpr/psum | solution.py:38
  281.5 9.1 %copy-start = (f32[64,32768]{1,0:T(8,128)S(1)}, f32[64,32768]{1,0:T(8,128)}, u32[]{:S(2)}) copy-start(f32[64,32768]{1,0:T(8,128)} %get-tuple-element.148) | copy-start | bytes 25165828 | tf_op jit(solution)/shard_map/while
  316.7 99.1 %all-reduce.5.cloned.1.call-start = ((), (), s32[]{:S(2)}) async-start(), calls=%async_computation.1 | async-start | bytes 262144 | tf_op jit(solution)/shard_map/while/body/eval_jaxpr/psum | solution.py:38
  416.8 90.3 %all-reduce.3.cloned.1.call-start = ((), (), s32[]{:S(2)}) async-start(), calls=%async_computation | async-start | bytes 262144 | tf_op jit(solution)/shard_map/while/body/eval_jaxpr/psum | solution.py:38
  416.8 9.1 %copy-start = (f32[64,32768]{1,0:T(8,128)S(1)}, f32[64,32768]{1,0:T(8,128)}, u32[]{:S(2)}) copy-start(f32[64,32768]{1,0:T(8,128)} %get-tuple-element.148) | copy-start | bytes 25165828 | tf_op jit(solution)/shard_map/while
  452.1 99.2 %all-reduce.5.cloned.1.call-start = ((), (), s32[]{:S(2)}) async-start(), calls=%async_computation.1 | async-start | bytes 262144 | tf_op jit(solution)/shard_map/while/body/eval_jaxpr/psum | solution.py:38
  552.3 0.7 copy-start.1
  552.3 0.7 copy-start.2
  552.3 0.7 copy-start.3
Sparse Core Ops, SparseCore 0:
  43.2 57.6 all-reduce.2
  103.7 41.2 all-reduce.4
  181.4 54.8 all-reduce.2
  239.1 41.2 all-reduce.4
  316.8 54.8 all-reduce.2
  374.5 41.2 all-reduce.4
  452.2 54.8 all-reduce.2
  510.0 41.2 all-reduce.4
